TPU v7x, 32 devices: a whole 2x2x4 slice. The times are simulated.
32 devices in a mesh: groups: 2 (over y), blk: 4 (over x, core), req: 4 (over z).
Axes of the slice: x: 2, y: 2, z: 4, core: 2. Of those that a mesh axis runs over, the one named last changes fastest.
Arguments:
- hidden_states: bfloat16 [640, 4608], P(('groups', 'req'), 'blk'), parts along dimension 0, may hold values from -12 to 12
- context_lengths: int32 [128], P(('groups', 'req')), parts along dimension 0, may hold values from 64 to 512
- cache_keys: bfloat16 [128, 512, 16, 128], P(('groups', 'req'), None, 'blk'), parts along dimension 0, may hold values from -1400 to 1400
- cache_values: bfloat16 [128, 512, 16, 128], P(('groups', 'req'), None, 'blk'), parts along dimension 0, may hold values from -6 to 6
- q_weight: bfloat16 [4608, 4096], P('req', 'blk'), may hold values from -0.09375 to 0.09375
- k_weight: bfloat16 [4608, 2048], P('req', 'blk'), may hold values from -0.09375 to 0.09375
- v_weight: bfloat16 [4608, 2048], P('req', 'blk'), may hold values from -0.09375 to 0.09375
- o_weight: bfloat16 [4096, 4608], P('blk'), may hold values from -1 to 1
- gate_weight: bfloat16 [18432, 4608], P(('blk', 'req')), may hold values from -0.09375 to 0.09375
- up_weight: bfloat16 [18432, 4608], P(('blk', 'req')), may hold values from -0.09375 to 0.09375
- down_weight: bfloat16 [18432, 4608], P(('blk', 'req')), may hold values from -0.0625 to 0.0625
- attn_gain: float32 [4608], P('blk'), may hold values from 0.1 to 1.9
- post_attn_gain: float32 [4608], P('blk'), may hold values from 0.1 to 1.9
- ffn_gain: float32 [4608], P('blk'), may hold values from 0.1 to 1.9
- post_ffn_gain: float32 [4608], P('blk'), may hold values from 0.1 to 1.9
Outputs:
- layer_output: bfloat16 [640, 4608], P(('groups', 'req'), 'blk'), parts along dimension 0
- draft_keys: bfloat16 [128, 5, 16, 128], P(('groups', 'req'), None, 'blk'), parts along dimension 0
- draft_values: bfloat16 [128, 5, 16, 128], P(('groups', 'req'), None, 'blk'), parts along dimension 0
There are 2 independent parts, one for each index of `groups`. A program takes and returns all parts, laid end to end along the dimension named above; an argument that names none is the same for every part. Nothing has to cross between parts.
All inputs are finite; a program needn't handle non-finite values.
Results may differ from a plain program's by a relative error of at most 0.015.
Values may be sent and summed in bfloat16 or wider, within the bound.
No kernel may reach another device: no remote copies, remote signals or barrier semaphores. Data moves between devices by JAX's collectives and lax.ppermute only.
A program may use at most 128 MiB of HBM per device.

v0:
```python
import jax
import jax.numpy as jnp
from jax import lax
from jax.sharding import PartitionSpec as P

D = 4608
HEADS = 32


EPSILON = 1e-06
NEGATIVE = -1e30


def rotate(values, positions):
    size = values.shape[-1]
    half = size // 2
    rates = 10000.0 ** (-(jnp.arange(half, dtype=jnp.float32) * 2.0) / size)
    angle = positions.astype(jnp.float32)[..., None] * rates
    cosine = jnp.cos(angle)
    sine = jnp.sin(angle)
    first = values[..., :half]
    second = values[..., half:]
    return jnp.concatenate(
        [first * cosine - second * sine, second * cosine + first * sine], axis=-1
    )


def scaling(total):
    return lax.rsqrt(total / D + EPSILON)[:, None]


def attend(queries, new_keys, new_values, cache_keys, cache_values, lengths):
    req_count, steps, heads, size = queries.shape
    shared = new_keys.shape[2]
    group = heads // shared
    scale = (D // HEADS) ** (-0.5)
    grouped = queries.reshape(req_count, steps, shared, group, size)
    older = (
        jnp.einsum("rskge,rcke->rkgsc", grouped, cache_keys, preferred_element_type=jnp.float32)
        * scale
    )
    newer = (
        jnp.einsum("rskge,rtke->rkgst", grouped, new_keys, preferred_element_type=jnp.float32)
        * scale
    )
    valid = jnp.arange(cache_keys.shape[1], dtype=jnp.int32)[None, :] < lengths[:, None]
    older = jnp.where(valid[:, None, None, None, :], older, NEGATIVE)
    causal = (
        jnp.arange(steps, dtype=jnp.int32)[:, None] >= jnp.arange(steps, dtype=jnp.int32)[None, :]
    )
    newer = jnp.where(causal, newer, NEGATIVE)
    highest = jnp.maximum(jnp.max(older, axis=-1), jnp.max(newer, axis=-1))[..., None]
    far_mass = jnp.exp(older - highest)
    near_mass = jnp.exp(newer - highest)
    total_mass = (jnp.sum(far_mass, axis=-1) + jnp.sum(near_mass, axis=-1))[..., None]
    far_weights = (far_mass / total_mass).astype(jnp.bfloat16)
    near_weights = (near_mass / total_mass).astype(jnp.bfloat16)
    blended = jnp.einsum(
        "rkgsc,rcke->rskge", far_weights, cache_values, preferred_element_type=jnp.float32
    )
    blended = blended + jnp.einsum(
        "rkgst,rtke->rskge", near_weights, new_values, preferred_element_type=jnp.float32
    )
    return blended.reshape(req_count * steps, heads * size).astype(jnp.bfloat16)


def body(
    hidden_states,
    context_lengths,
    cache_keys,
    cache_values,
    q_weight,
    k_weight,
    v_weight,
    o_weight,
    gate_weight,
    up_weight,
    down_weight,
    attn_gain,
    post_attn_gain,
    ffn_gain,
    post_ffn_gain,
):
    token_rows = hidden_states.shape[0]
    req_count = context_lengths.shape[0]
    steps = token_rows // req_count
    kv_local = cache_keys.shape[2]
    size = cache_keys.shape[3]
    query_cols = q_weight.shape[1]
    key_cols = k_weight.shape[1]
    heads_local = query_cols // size
    states = hidden_states.astype(jnp.float32)
    total = lax.psum(jnp.sum(states * states, axis=1), "blk")
    normed = (states * scaling(total) * attn_gain).astype(jnp.bfloat16)
    whole = lax.all_gather(normed, "blk", axis=1, tiled=True)
    slices = lax.all_to_all(whole, "req", split_axis=1, concat_axis=0, tiled=True)
    joined = lax.psum_scatter(
        jnp.concatenate(
            [
                jnp.dot(slices, q_weight, preferred_element_type=jnp.float32),
                jnp.dot(slices, k_weight, preferred_element_type=jnp.float32),
                jnp.dot(slices, v_weight, preferred_element_type=jnp.float32),
            ],
            axis=1,
        ),
        "req",
        scatter_dimension=0,
        tiled=True,
    )
    query_lin = joined[:, :query_cols]
    key_lin = joined[:, query_cols : query_cols + key_cols]
    value_lin = joined[:, query_cols + key_cols :]
    positions = (context_lengths[:, None] + jnp.arange(steps, dtype=jnp.int32)[None, :]).reshape(
        token_rows
    )
    queries = rotate(query_lin.reshape(token_rows, heads_local, size), positions[:, None]).astype(
        jnp.bfloat16
    )
    new_keys = rotate(key_lin.reshape(token_rows, kv_local, size), positions[:, None]).astype(
        jnp.bfloat16
    )
    draft_keys = new_keys.reshape(req_count, steps, kv_local, size)
    draft_values = value_lin.astype(jnp.bfloat16).reshape(req_count, steps, kv_local, size)
    attended = attend(
        queries.reshape(req_count, steps, heads_local, size),
        draft_keys,
        draft_values,
        cache_keys,
        cache_values,
        context_lengths,
    )
    mixed = (
        lax.psum_scatter(
            lax.dot_general(
                o_weight, attended, (((0,), (1,)), ((), ())), preferred_element_type=jnp.float32
            ).astype(jnp.bfloat16),
            "blk",
            scatter_dimension=0,
            tiled=True,
        )
        .astype(jnp.float32)
        .T
    )
    total = lax.psum(jnp.sum(mixed * mixed, axis=1), "blk")
    middle = (states + mixed * scaling(total) * post_attn_gain).astype(jnp.bfloat16)
    middle_wide = middle.astype(jnp.float32)
    total = lax.psum(jnp.sum(middle_wide * middle_wide, axis=1), "blk")
    normed_mid = (middle_wide * scaling(total) * ffn_gain).astype(jnp.bfloat16)
    features = lax.all_gather(normed_mid, "blk", axis=1, tiled=True)
    piece = lax.all_gather(features, "req", axis=0, tiled=True)
    gate = lax.dot_general(
        piece, gate_weight, (((1,), (1,)), ((), ())), preferred_element_type=jnp.float32
    )
    up = lax.dot_general(
        piece, up_weight, (((1,), (1,)), ((), ())), preferred_element_type=jnp.float32
    )
    terms = lax.dot_general(
        down_weight,
        (jax.nn.gelu(gate, approximate=True) * up).astype(jnp.bfloat16),
        (((0,), (1,)), ((), ())),
        preferred_element_type=jnp.float32,
    )
    partial_sum = lax.psum_scatter(
        terms.astype(jnp.bfloat16), "blk", scatter_dimension=0, tiled=True
    )
    ffn_out = (
        lax.psum_scatter(partial_sum, "req", scatter_dimension=1, tiled=True).astype(jnp.float32).T
    )
    total = lax.psum(jnp.sum(ffn_out * ffn_out, axis=1), "blk")
    layer_output = (middle_wide + ffn_out * scaling(total) * post_ffn_gain).astype(jnp.bfloat16)
    return (layer_output, draft_keys, draft_values)


def solution(mesh):
    placed = (
        P(("groups", "req"), "blk"),
        P(("groups", "req")),
        P(("groups", "req"), None, "blk", None),
        P(("groups", "req"), None, "blk", None),
        P("req", "blk"),
        P("req", "blk"),
        P("req", "blk"),
        P("blk", None),
        P(("blk", "req"), None),
        P(("blk", "req"), None),
        P(("blk", "req"), None),
        P("blk"),
        P("blk"),
        P("blk"),
        P("blk"),
    )
    return jax.shard_map(
        body,
        mesh=mesh,
        in_specs=placed,
        out_specs=(
            P(("groups", "req"), "blk"),
            P(("groups", "req"), None, "blk", None),
            P(("groups", "req"), None, "blk", None),
        ),
        check_vma=False,
    )
```

profile of v0, /device:TPU:0, one launch (start us, length us, event | category | flops | bytes accessed | tf_op | source)
XLA Modules:
  0.0 343.2 jit_solution(14080741423998053400)
XLA Ops:
  7.2 1.2 fusion.35
  8.4 8.4 %psum.28 = f32[80]{0:T(128)S(1)} all-reduce(f32[80]{0:T(128)S(1)} %fusion.35), channel_id=1, replica_groups=mesh['groups'=2,'blk'=4,'req'=4] {'blk'}, use_global_device_ids=true, to_apply=%region_1.0 | all-reduce | flops 80 | bytes 640 | tf_op jit(solution)/shard_map/psum | solution.py:93
  16.8 1.1 fusion.37
  18.0 7.2 %all_gather.9 = bf16[80,4608]{1,0:T(8,128)(2,1)S(1)} all-gather(bf16[80,1152]{1,0:T(8,128)(2,1)S(1)} %fusion.37), channel_id=1, replica_groups=mesh['groups'=2,'blk'=4,'req'=4] {'blk'}, dimensions={1}, use_global_device_ids=true | all-gather | bytes 921600 | tf_op jit(solution)/shard_map/all_gather | solution.py:95
  25.2 24.5 %all_to_all.19 = bf16[80,4,1152]{2,0,1:T(8,128)(2,1)S(1)} all-to-all(bf16[80,4,1152]{2,0,1:T(8,128)(2,1)S(1)} %bitcast.84), channel_id=1, replica_groups=mesh['groups'=2,'blk'=4,'req'=4] {'req'}, dimensions={1} | all-to-all | bytes 1474560 | tf_op jit(solution)/shard_map/all_to_all | solution.py:96
  51.0 1.0 fusion.53
  52.0 1.7 pad_maximum_fusion
  54.8 50.5 %reduce-scatter.9.cloned.1.call-done = f32[80,2048]{1,0:T(8,128)} async-done(((f32[320,2048]{1,0:T(8,128)}), f32[80,2048]{1,0:T(8,128)}) %reduce-scatter.9.cloned.1.call-update) | async-done | bytes 655376 | tf_op jit(solution)/shard_map/reduce_scatter | solution.py:97
  106.3 1.0 slice_bitcast_fusion
  107.4 0.9 slice.32
  109.1 1.4 fusion.52
  110.5 6.0 %bitcast_reduce_fusion = (f32[16,4,2,5]{3,2,1,0:T(2,128)S(1)}, f32[16,4,5,2,512]{4,2,3,1,0:T(8,128)S(1)}) fusion(pred[16,512]{1,0:T(8,128)(4,1)S(1)} %iota_compare_fusion, bf16[16,512,4,128,1]{3,2,1,0,4:T(4,128)(2,1)} %bitcast.79, bf16[16,5,4,2,64]{4,1,3,2,0:T(8,128)(2,1)S(1)} %copy.57, bf16[16,5,4,2,64]{4,1,3,2,0:T(8,128)(2,1)S(1)} %copy.56), kind=kOutput, calls=%fused_computation.13 | convolution fusion | flops 85196160 | bytes 9873920 | tf_op jit(solution)/shard_map/rskge,rcke->rkgsc/dot_general | solution.py:39
  116.8 1.0 fusion.8
  117.9 2.0 fusion.16
  120.5 5.4 %fusion.5 = bf16[4608,80]{0,1:T(8,128)(2,1)S(1)} fusion(bf16[80,1024]{1,0:T(8,128)(2,1)S(1)} %convert_element_type.76, bf16[1024,4608]{1,0:T(8,128)(2,1)} %param.22), kind=kOutput, calls=%fused_computation.7 | convolution fusion | flops 755343360 | bytes 10338304 | tf_op jit(solution)/shard_map/dot_general | solution.py:134
  125.9 1.4 copy.77
  127.4 25.3 %reduce-scatter.13.cloned.1.call-done = bf16[1152,80]{1,0:T(8,128)(2,1)} async-done(((bf16[4608,80]{1,0:T(8,128)(2,1)}), bf16[1152,80]{1,0:T(8,128)(2,1)}) %reduce-scatter.13.cloned.1.call-update) | async-done | bytes 184336
  152.6 1.1 copy.78
  153.9 5.8 %psum.29 = f32[80]{0:T(128)S(1)} all-reduce(f32[80]{0:T(128)S(1)} %fusion.29), channel_id=1, replica_groups=mesh['groups'=2,'blk'=4,'req'=4] {'blk'}, use_global_device_ids=true, to_apply=%region_9.10 | all-reduce | flops 80 | bytes 640 | tf_op jit(solution)/shard_map/psum | solution.py:144
  159.9 5.7 %psum.30 = f32[80]{0:T(128)S(1)} all-reduce(f32[80]{0:T(128)S(1)} %get-tuple-element.18), channel_id=1, replica_groups=mesh['groups'=2,'blk'=4,'req'=4] {'blk'}, use_global_device_ids=true, to_apply=%region_11.12 | all-reduce | flops 80 | bytes 640 | tf_op jit(solution)/shard_map/psum | solution.py:147
  165.7 8.9 %all_gather.10 = bf16[80,4608]{1,0:T(8,128)(2,1)} all-gather(bf16[80,1152]{1,0:T(8,128)(2,1)S(1)} %fusion.41), channel_id=1, replica_groups=mesh['groups'=2,'blk'=4,'req'=4] {'blk'}, dimensions={1}, use_global_device_ids=true | all-gather | bytes 921600 | tf_op jit(solution)/shard_map/all_gather | solution.py:149
  174.7 60.7 %all-gather.2.cloned.1.call-done = bf16[320,4608]{1,0:T(8,128)(2,1)} async-done(((bf16[80,4608]{1,0:T(8,128)(2,1)}), bf16[320,4608]{1,0:T(8,128)(2,1)}) %all-gather.2.cloned.1.call-update) | async-done | bytes 2949136 | tf_op jit(solution)/shard_map/all_gather | solution.py:150
  235.3 9.0 %fusion.56 = f32[320,1152]{1,0:T(8,128)S(1)} fusion(bf16[320,4608]{1,0:T(8,128)(2,1)} %all-gather.2.cloned.1.call-done, bf16[1152,4608]{1,0:T(8,128)(2,1)} %param.23), kind=kOutput, calls=%fused_computation.95 | convolution fusion | flops 3397386240 | bytes 15040512 | tf_op jit(solution)/shard_map/dot_general | solution.py:151
  244.4 8.2 %fusion.6 = bf16[320,1152]{1,0:T(8,128)(2,1)S(1)} fusion(bf16[320,4608]{1,0:T(8,128)(2,1)S(1)} %copy-done.10, bf16[1152,4608]{1,0:T(8,128)(2,1)} %param.24, f32[320,1152]{1,0:T(8,128)S(1)} %fusion.56), kind=kOutput, calls=%fused_computation.9 | convolution fusion | flops 3401072640 | bytes 15777792 | tf_op jit(solution)/shard_map/dot_general | solution.py:154
  252.7 5.3 %fusion.4 = bf16[4608,320]{0,1:T(8,128)(2,1)} fusion(bf16[320,1152]{1,0:T(8,128)(2,1)S(1)} %fusion.6, bf16[1152,4608]{1,0:T(8,128)(2,1)S(1)} %bitcast.92), kind=kOutput, calls=%fused_computation.5 | convolution fusion | flops 3398860800 | bytes 14303232 | tf_op jit(solution)/shard_map/dot_general | solution.py:157
  258.0 5.5 %copy.79 = bf16[4608,320]{1,0:T(8,128)(2,1)} copy(bf16[4608,320]{0,1:T(8,128)(2,1)} %fusion.4) | data formatting | bytes 5898240
  263.6 39.1 %reduce-scatter.15.cloned.1.call-done = bf16[1152,320]{1,0:T(8,128)(2,1)} async-done(((bf16[4608,320]{1,0:T(8,128)(2,1)}), bf16[1152,320]{1,0:T(8,128)(2,1)}) %reduce-scatter.15.cloned.1.call-update) | async-done | bytes 737296
  302.7 2.2 copy.80
  305.6 22.6 %reduce-scatter.11.cloned.1.call-done = bf16[1152,80]{0,1:T(8,128)(2,1)} async-done(((bf16[1152,320]{0,1:T(8,128)(2,1)}), bf16[1152,80]{0,1:T(8,128)(2,1)}) %reduce-scatter.11.cloned.1.call-update) | async-done | bytes 184336 | tf_op jit(solution)/shard_map/reduce_scatter | solution.py:167
  328.2 1.1 fusion.32
  329.3 5.7 %psum.31 = f32[80]{0:T(128)S(1)} all-reduce(f32[80]{0:T(128)S(1)} %fusion.32), channel_id=1, replica_groups=mesh['groups'=2,'blk'=4,'req'=4] {'blk'}, use_global_device_ids=true, to_apply=%region_15.16 | all-reduce | flops 80 | bytes 640 | tf_op jit(solution)/shard_map/psum | solution.py:169
  334.9 1.7 fusion.42
  (78 shorter events, 6.5 us)
Async XLA Ops:
  7.2 43.8 %copy-start = (bf16[1152,1024]{1,0:T(8,128)(2,1)S(1)}, bf16[1152,1024]{1,0:T(8,128)(2,1)}, u32[]{:S(2)}) copy-start(bf16[1152,1024]{1,0:T(8,128)(2,1)} %param.19) | copy-start | bytes 7077892
  7.2 98.1 %reduce-scatter.9.cloned.1.call-start = ((), (), s32[]{:S(2)}) async-start(), calls=%async_computation.5 | async-start | bytes 3276800 | tf_op jit(solution)/shard_map/reduce_scatter | solution.py:97
  16.8 32.9 %copy-start.3 = (bf16[1152,512]{1,0:T(8,128)(2,1)S(1)}, bf16[1152,512]{1,0:T(8,128)(2,1)}, u32[]{:S(2)}) copy-start(bf16[1152,512]{1,0:T(8,128)(2,1)} %param.21) | copy-start | bytes 3538948
  25.2 25.1 %copy-start.4 = (bf16[1152,512]{1,0:T(8,128)(2,1)S(1)}, bf16[1152,512]{1,0:T(8,128)(2,1)}, u32[]{:S(2)}) copy-start(bf16[1152,512]{1,0:T(8,128)(2,1)} %param.20) | copy-start | bytes 3538948
  53.7 0.7 copy-start.9
  53.7 98.9 %reduce-scatter.13.cloned.1.call-start = ((), (), s32[]{:S(2)}) async-start(), calls=%async_computation.8 | async-start | bytes 1474560
  106.3 13.6 %copy-start.5 = (bf16[16,5,4,128]{3,2,1,0:T(4,128)(2,1)}, bf16[16,5,4,128]{3,2,1,0:T(4,128)(2,1)S(1)}, u32[]{:S(2)}) copy-start(bf16[16,5,4,128]{3,2,1,0:T(4,128)(2,1)S(1)} %reshape.149) | copy-start | bytes 245764
  109.1 8.8 %slice-start.3 = ((s8[8388608]{0:T(1024)(128)(4,1)}), s8[4194304]{0:T(1024)(128)(4,1)S(1)}, s32[]{:S(2)}) async-start(s8[8388608]{0:T(1024)(128)(4,1)} %bitcast.93), calls=%async_computation.13 | async-start | bytes 8388608
  110.5 7.4 %slice-start.4 = ((s8[8388608]{0:T(1024)(128)(4,1)}), s8[4194304]{0:T(1024)(128)(4,1)S(1)}, s32[]{:S(2)}) async-start(s8[8388608]{0:T(1024)(128)(4,1)} %bitcast.93), calls=%async_computation.14 | async-start | bytes 8388608
  125.9 33.8 %copy-start.2 = (bf16[80,1152]{1,0:T(8,128)(2,1)S(1)}, bf16[80,1152]{1,0:T(8,128)(2,1)}, u32[]{:S(2)}) copy-start(bf16[80,1152]{1,0:T(8,128)(2,1)} %param.15) | copy-start | bytes 552964
  125.9 33.8 %copy-start.6 = (f32[1152]{0:T(1024)S(1)}, f32[1152]{0:T(1024)}, u32[]{:S(2)}) copy-start(f32[1152]{0:T(1024)} %param.27) | copy-start | bytes 13828
  125.9 39.7 %copy-start.8 = (f32[1152]{0:T(1024)S(1)}, f32[1152]{0:T(1024)}, u32[]{:S(2)}) copy-start(f32[1152]{0:T(1024)} %param.28) | copy-start | bytes 13828
  127.3 108.0 %all-gather.2.cloned.1.call-start = ((), (), s32[]{:S(2)}) async-start(), calls=%async_computation.6 | async-start | bytes 3686400 | tf_op jit(solution)/shard_map/all_gather | solution.py:150
  174.6 128.1 %reduce-scatter.15.cloned.1.call-start = ((), (), s32[]{:S(2)}) async-start(), calls=%async_computation.9 | async-start | bytes 4423680
  235.3 9.0 %copy-start.10 = (bf16[320,4608]{1,0:T(8,128)(2,1)S(1)}, bf16[320,4608]{1,0:T(8,128)(2,1)}, u32[]{:S(2)}) copy-start(bf16[320,4608]{1,0:T(8,128)(2,1)} %all-gather.2.cloned.1.call-done) | copy-start | bytes 8847364
  235.3 17.3 %slice-start = ((s8[10616832]{0:T(1024)(128)(4,1)}), s8[4194304]{0:T(1024)(128)(4,1)S(1)}, s32[]{:S(2)}) async-start(s8[10616832]{0:T(1024)(128)(4,1)} %bitcast.91), calls=%async_computation.10 | async-start | bytes 8388608
  235.3 17.3 %slice-start.1 = ((s8[10616832]{0:T(1024)(128)(4,1)}), s8[4194304]{0:T(1024)(128)(4,1)S(1)}, s32[]{:S(2)}) async-start(s8[10616832]{0:T(1024)(128)(4,1)} %bitcast.91), calls=%async_computation.11 | async-start | bytes 8388608
  244.4 8.3 %slice-start.2 = ((s8[10616832]{0:T(1024)(128)(4,1)}), s8[2228224]{0:T(1024)(128)(4,1)S(1)}, s32[]{:S(2)}) async-start(s8[10616832]{0:T(1024)(128)(4,1)} %bitcast.91), calls=%async_computation.12 | async-start | bytes 4456448
  263.6 71.4 %copy-start.7 = (f32[1152]{0:T(1024)S(1)}, f32[1152]{0:T(1024)}, u32[]{:S(2)}) copy-start(f32[1152]{0:T(1024)} %param.29) | copy-start | bytes 13828
  263.6 73.1 %copy-start.1 = (bf16[1152,1024]{1,0:T(8,128)(2,1)S(1)}, bf16[1152,1024]{1,0:T(8,128)(2,1)}, u32[]{:S(2)}) copy-start(bf16[1152,1024]{1,0:T(8,128)(2,1)} %param.19) | copy-start | bytes 7077892
  263.6 64.6 %reduce-scatter.11.cloned.1.call-start = ((), (), s32[]{:S(2)}) async-start(), calls=%async_computation.7 | async-start | bytes 921600 | tf_op jit(solution)/shard_map/reduce_scatter | solution.py:167
Sparse Core Ops, SparseCore 0:
  53.8 51.4 reduce-scatter.8
  127.4 25.1 reduce-scatter.12
  174.7 60.5 all-gather.1
  263.7 39.0 reduce-scatter.14
  305.1 23.0 reduce-scatter.10
where the time goes:
time: 344 us; the launch traced here: 343 us
  waiting for transfers between devices  198 us (58%)
  blocking collectives  66 us (19%)
  matrix products  39.9 us (12%)
  local copies, waits for them, and re-layouts  15.1 us (4%)
  between operations  14.2 us (4%)
  other arithmetic  9.58 us (3%)
    unnamed x7, waiting for transfers between devices  64.5 us
    all_gather x1, waiting for transfers between devices, body(): piece = lax.all_gather(features, 'req', axis=0, tiled=True)  60.7 us
    reduce_scatter x1, waiting for transfers between devices, body(): lax.psum_scatter(jnp.concatenate([jnp.dot(slices, q_weight, preferred_ele...  50.5 us
    all_to_all x1, blocking collectives, body(): lax.all_to_all(whole, 'req', split_axis=1, concat_axis=0, tiled=True)  24.5 us
    reduce_scatter x1, waiting for transfers between devices, body(): lax.psum_scatter(partial_sum, 'req', scatter_dimension=1, tiled=True)  22.6 us
    unnamed x39, local copies, waits for them, and re-layouts  12.6 us
    dot_general x1, matrix products, body(): lax.dot_general(piece, gate_weight, (((1,), (1,)), ((), ())), preferred_e...  9.03 us
    all_gather x1, blocking collectives, body(): features = lax.all_gather(normed_mid, 'blk', axis=1, tiled=True)  8.85 us
  transfers between devices with their start and end apart: 5, of which 5 were waited for; matrix products, arithmetic and copies ran while one was open for 0% of the time, Pallas kernels for 0%

commit v1 on v0

v1 whole, which is shorter than its diff:
```python
import functools

import jax
import jax.numpy as jnp
from jax import lax
from jax.experimental import pallas as pl
from jax.experimental.pallas import tpu as pltpu
from jax.sharding import PartitionSpec as P

D = 4608
HEADS = 32


EPSILON = 1e-06
NEGATIVE = -1e30
VMEM = pltpu.VMEM
GRANT = 4 << 20


def scaling(total):
    return lax.rsqrt(total / D + EPSILON)[:, None]


def angles(positions, size):
    half = size // 2
    rates = 10000.0 ** (-(jnp.arange(half, dtype=jnp.float32) * 2.0) / size)
    angle = positions.astype(jnp.float32)[:, None] * rates
    cosine = jnp.cos(angle)
    sine = jnp.sin(angle)
    return (
        jnp.concatenate([cosine, cosine], axis=1),
        jnp.concatenate([-sine, sine], axis=1),
    )


def fetch_kernel(pieces, *refs):
    count = len(refs) // 2
    sems = refs[-1]
    copies = []
    for i in range(count):
        rows = refs[i].shape[0] // pieces
        for at in range(pieces):
            part = pl.ds(at * rows, rows)
            copies.append(
                pltpu.make_async_copy(
                    refs[i].at[part], refs[count + i].at[part], sems.at[i * pieces + at]
                )
            )
    for copy in copies:
        copy.start()
    for copy in copies:
        copy.wait()


def fetch(*arrays):
    pieces = 4 if all(a.ndim == 3 or a.shape[0] % 64 == 0 for a in arrays) else 1
    size = sum(a.size * a.dtype.itemsize for a in arrays)
    return pl.pallas_call(
        functools.partial(fetch_kernel, pieces),
        out_shape=[pltpu.VMEM(a.shape, a.dtype) for a in arrays],
        in_specs=[pl.BlockSpec(memory_space=pltpu.HBM)] * len(arrays),
        out_specs=[pl.BlockSpec(memory_space=VMEM)] * len(arrays),
        scratch_shapes=[pltpu.SemaphoreType.DMA((len(arrays) * pieces,))],
        compiler_params=pltpu.CompilerParams(vmem_limit_bytes=1 << 20),
        cost_estimate=pl.CostEstimate(flops=size * 300, bytes_accessed=size, transcendentals=0),
        name="fetch",
    )(*arrays)


def add_kernel(*refs):
    total = refs[0][...].astype(jnp.float32)
    for ref in refs[1:-1]:
        total = total + ref[...].astype(jnp.float32)
    refs[-1][...] = total.astype(refs[-1].dtype)


def add_part(wholes, index, parts, rows, dtype):
    width = wholes[0].shape[1]
    if rows % 8:
        total = sum(
            [w[index * rows : (index + 1) * rows].astype(jnp.float32) for w in wholes]
            + [p.astype(jnp.float32) for p in parts]
        )
        return total.astype(dtype)
    return pl.pallas_call(
        add_kernel,
        grid=(1,),
        in_specs=[pl.BlockSpec((rows, width), lambda i: (index, 0))] * len(wholes)
        + [pl.BlockSpec((rows, width), lambda i: (0, 0))] * len(parts),
        out_specs=pl.BlockSpec((rows, width), lambda i: (0, 0)),
        out_shape=jax.ShapeDtypeStruct((rows, width), dtype),
        compiler_params=pltpu.CompilerParams(vmem_limit_bytes=8 << 20),
        name="add_part",
    )(*wholes, *parts)


def project_kernel(parts, own_ref, x_ref, q_ref, k_ref, v_ref, *rest):
    outs, scaled = rest[:parts], rest[parts]
    rows = x_ref.shape[0] // parts
    for part in range(parts):
        source = lax.rem(own_ref[0] + part, parts)
        scaled[part * rows : (part + 1) * rows, :] = x_ref[
            pl.ds(pl.multiple_of(source * rows, 8), rows), :
        ]
    start = 0
    for weight in (q_ref, k_ref, v_ref):
        width = weight.shape[1]
        product = jnp.dot(scaled[...], weight[...], preferred_element_type=jnp.float32)
        for part in range(parts):
            outs[part][:, start : start + width] = product[
                part * rows : (part + 1) * rows
            ].astype(jnp.bfloat16)
        start += width


def project(own, x, q_weight, k_weight, v_weight, parts):
    rows = x.shape[0] // parts
    width = q_weight.shape[1] + k_weight.shape[1] + v_weight.shape[1]
    spec = pl.BlockSpec(memory_space=VMEM)
    return pl.pallas_call(
        functools.partial(project_kernel, parts),
        out_shape=[jax.ShapeDtypeStruct((rows, width), jnp.bfloat16)] * parts,
        in_specs=[pl.BlockSpec(memory_space=pltpu.SMEM)] + [spec] * 4,
        out_specs=[spec] * parts,
        scratch_shapes=[VMEM(x.shape, jnp.bfloat16)],
        compiler_params=pltpu.CompilerParams(vmem_limit_bytes=24 << 20),
        cost_estimate=pl.CostEstimate(
            flops=2 * x.shape[0] * x.shape[1] * width,
            bytes_accessed=2 * x.shape[1] * width,
            transcendentals=0,
        ),
        name="project",
    )(own, x, q_weight, k_weight, v_weight)


def attend_kernel(parts, req_count, kv_count, scale, *refs):
    lengths = refs[0]
    pieces = refs[1 : 1 + parts]
    (row_scale, cosine, sine, keys, values, attended, new_keys, new_values) = refs[
        1 + parts : 9 + parts
    ]
    flat, lin, mixed, packed, code = refs[9 + parts :]
    step = pl.program_id(0)
    rows, width = pieces[0].shape
    steps = rows // req_count
    size = keys.shape[-1]
    kv_width = kv_count * size
    q_width = width - 2 * kv_width
    heads = q_width // size
    group = heads // kv_count
    slots = keys.shape[1]
    shift = kv_count.bit_length() - 1

    @pl.when(step == 0)
    def _():
        total = pieces[0][...].astype(jnp.float32)
        for piece in pieces[1:]:
            total = total + piece[...].astype(jnp.float32)
        total = total * row_scale[...]
        for at in range((q_width + kv_width) // size):
            lanes = slice(at * size, (at + 1) * size)
            vector = total[:, lanes]
            turned = (
                vector * cosine[...] + pltpu.roll(vector, size // 2, 1) * sine[...]
            ).astype(jnp.bfloat16)
            flat[:rows, lanes] = turned.astype(jnp.float32)
            if at >= heads:
                new_keys[:, (at - heads) * size : (at - heads + 1) * size] = turned
        plain = total[:, q_width + kv_width :].astype(jnp.bfloat16)
        new_values[...] = plain
        flat[:rows, q_width + kv_width :] = plain.astype(jnp.float32)
        flat[rows:, :] = jnp.zeros((flat.shape[0] - rows, width), jnp.float32)
        for at in range(req_count):
            lin[at * 8 : (at + 1) * 8, :] = flat[at * steps : at * steps + 8, :]
        row = lax.broadcasted_iota(jnp.int32, code.shape, 0)
        column = lax.broadcasted_iota(jnp.int32, code.shape, 1)
        owner = jnp.right_shift(row, 3)
        shared = jnp.zeros_like(owner)
        for head in range(heads):
            shared = jnp.where(owner == head, head // group, shared)
        code[...] = jnp.where(
            jnp.bitwise_and(column, kv_count - 1) == shared,
            jnp.right_shift(column, shift),
            jnp.int32(1 << 30),
        )

    base = q_width + kv_width
    dims = (((1,), (1,)), ((), ()))
    factor = scale * 1.4426950408889634
    row = lax.broadcasted_iota(jnp.int32, (heads * 8, kv_count * 8), 0)
    column = lax.broadcasted_iota(jnp.int32, (heads * 8, kv_count * 8), 1)
    owner = jnp.right_shift(row, 3)
    shared = jnp.zeros_like(owner)
    for head in range(heads):
        shared = jnp.where(owner == head, head // group, shared)
    draft = jnp.bitwise_and(column, 7)
    allowed = (
        (jnp.right_shift(column, 3) == shared)
        & (draft <= jnp.bitwise_and(row, 7))
        & (draft < steps)
    )

    def one(request, taken):
        first = pl.multiple_of(request * 8, 8)
        now = lin[pl.ds(first, 8), :]

        def stacked(start, count):
            return jnp.concatenate(
                [now[:, start + i * size : start + (i + 1) * size] for i in range(count)], axis=0
            ).astype(jnp.bfloat16)

        query = stacked(0, heads)
        older = lax.dot_general(
            query, keys[request, :taken], dims, preferred_element_type=jnp.float32
        )
        older = jnp.where(code[:, :taken] < lengths[request], older, NEGATIVE)
        newer = lax.dot_general(
            query, stacked(q_width, kv_count), dims, preferred_element_type=jnp.float32
        )
        newer = jnp.where(allowed, newer, NEGATIVE)
        highest = jnp.maximum(
            jnp.max(older, axis=1, keepdims=True), jnp.max(newer, axis=1, keepdims=True)
        )
        far = jnp.exp2((older - highest) * factor)
        near = jnp.exp2((newer - highest) * factor)
        mass = jnp.sum(far, axis=1, keepdims=True) + jnp.sum(near, axis=1, keepdims=True)
        blended = jnp.dot(
            far.astype(jnp.bfloat16), values[request, :taken], preferred_element_type=jnp.float32
        )
        blended = blended + jnp.dot(
            near.astype(jnp.bfloat16), stacked(base, kv_count), preferred_element_type=jnp.float32
        )
        blended = blended / mass
        for h in range(heads):
            mixed[pl.ds(first, 8), h * size : (h + 1) * size] = blended[h * 8 : (h + 1) * 8]

    together = 2 if req_count % 2 == 0 else 1
    needed = lengths[step * together]
    for i in range(1, together):
        needed = jnp.maximum(needed, lengths[step * together + i])
    chunks = 4 if (slots // kv_count) % 4 == 0 else 1
    span = slots // kv_count // chunks
    for chunk in range(chunks):
        fits = needed > chunk * span
        if chunk < chunks - 1:
            fits = fits & (needed <= (chunk + 1) * span)

        @pl.when(fits)
        def _(chunk=chunk):
            for i in range(together):
                one(step * together + i, (chunk + 1) * span * kv_count)

    @pl.when(step == req_count // together - 1)
    def _():
        for at in range(req_count):
            packed[at * steps : (at + 1) * steps, :] = mixed[at * 8 : at * 8 + steps, :]
        attended[...] = packed[...].astype(jnp.bfloat16)


def attend(lengths, pieces, row_scale, cosine, sine, keys, values, kv_count):
    rows, width = pieces[0].shape
    req_count, slots, size = keys.shape
    kv_width = kv_count * size
    heads = (width - 2 * kv_width) // size
    spec = pl.BlockSpec(memory_space=VMEM)
    whole = lambda shape: pl.BlockSpec(shape, lambda i, n: (0,) * len(shape))
    return pl.pallas_call(
        functools.partial(
            attend_kernel, len(pieces), req_count, kv_count, (D // HEADS) ** (-0.5)
        ),
        grid_spec=pltpu.PrefetchScalarGridSpec(
            num_scalar_prefetch=1,
            grid=(req_count // 2 if req_count % 2 == 0 else req_count,),
            in_specs=[whole(p.shape) for p in pieces]
            + [
                whole(row_scale.shape),
                whole(cosine.shape),
                whole(sine.shape),
                spec,
                spec,
            ],
            out_specs=[
                whole((rows, heads * size)),
                whole((rows, kv_width)),
                whole((rows, kv_width)),
            ],
            scratch_shapes=[
                VMEM((rows + 8, width), jnp.float32),
                VMEM((req_count * 8, width), jnp.float32),
                VMEM((req_count * 8, heads * size), jnp.float32),
                VMEM((rows, heads * size), jnp.float32),
                VMEM((heads * 8, slots), jnp.int32),
            ],
        ),
        out_shape=[
            jax.ShapeDtypeStruct((rows, heads * size), jnp.bfloat16),
            jax.ShapeDtypeStruct((rows, kv_width), jnp.bfloat16),
            jax.ShapeDtypeStruct((rows, kv_width), jnp.bfloat16),
        ],
        compiler_params=pltpu.CompilerParams(vmem_limit_bytes=6 << 20),
        cost_estimate=pl.CostEstimate(
            flops=4 * req_count * heads * 8 * slots * size,
            bytes_accessed=4 * req_count * slots * size,
            transcendentals=req_count * heads * 8 * slots,
        ),
        name="attend",
    )(lengths, *pieces, row_scale, cosine, sine, keys, values)


def half_kernel(block, half_ref, a_ref, w_ref, out_ref):
    width = out_ref.shape[1]
    first = half_ref[0] * width
    if len(a_ref.shape) == 2:
        a = a_ref[...]
    else:
        a = jnp.concatenate([a_ref[i] for i in range(a_ref.shape[0])], axis=1)
    for at in range(width // block):
        lanes = pl.ds(pl.multiple_of(first + at * block, 128), block)
        out_ref[:, at * block : (at + 1) * block] = jnp.dot(
            a, w_ref[:, lanes], preferred_element_type=jnp.float32
        ).astype(out_ref.dtype)


def half_product(half, a, weight, dtype):
    rows, depth = a.shape[-2], weight.shape[0]
    width = weight.shape[1] // 2
    block = 256 if width % 256 == 0 else 128
    spec = pl.BlockSpec(memory_space=VMEM)
    return pl.pallas_call(
        functools.partial(half_kernel, block),
        in_specs=[pl.BlockSpec(memory_space=pltpu.SMEM), spec, spec],
        out_specs=spec,
        out_shape=jax.ShapeDtypeStruct((rows, width), dtype),
        compiler_params=pltpu.CompilerParams(vmem_limit_bytes=GRANT),
        cost_estimate=pl.CostEstimate(
            flops=2 * rows * depth * width,
            bytes_accessed=2 * depth * width,
            transcendentals=0,
        ),
        name="half_product",
    )(half, a, weight)


def hidden_kernel(block, core_ref, own_ref, other_ref, gate_ref, up_ref, out_ref):
    width = own_ref.shape[1]
    units = gate_ref.shape[0]
    core = core_ref[0]
    dims = (((1,), (1,)), ((), ()))

    def step(at, carry):
        rows = pl.ds(pl.multiple_of(at * block, 8), block)

        def columns(half):
            lanes = pl.ds(pl.multiple_of(half * width, 128), width)
            return jnp.concatenate([gate_ref[rows, lanes], up_ref[rows, lanes]], axis=0)

        both = lax.dot_general(
            own_ref[...], columns(core), dims, preferred_element_type=jnp.float32
        ) + lax.dot_general(
            other_ref[...], columns(1 - core), dims, preferred_element_type=jnp.float32
        )
        out_ref[at] = (
            jax.nn.gelu(both[:, :block], approximate=True) * both[:, block:]
        ).astype(jnp.bfloat16)
        return carry

    lax.fori_loop(0, units // block, step, 0)


def hidden_units(core, own, other, gate_weight, up_weight):
    rows, width = own.shape
    units, depth = gate_weight.shape
    block = 128 if units % 128 == 0 else units
    count = units // block
    spec = pl.BlockSpec(memory_space=VMEM)
    return pl.pallas_call(
        functools.partial(hidden_kernel, block),
        in_specs=[pl.BlockSpec(memory_space=pltpu.SMEM), spec, spec, spec, spec],
        out_specs=spec,
        out_shape=jax.ShapeDtypeStruct((count, rows, block), jnp.bfloat16),
        compiler_params=pltpu.CompilerParams(vmem_limit_bytes=GRANT),
        cost_estimate=pl.CostEstimate(
            flops=4 * rows * depth * units,
            bytes_accessed=4 * depth * units,
            transcendentals=rows * units,
        ),
        name="hidden_units",
    )(core, own, other, gate_weight, up_weight)


def body(
    hidden_states,
    context_lengths,
    cache_keys,
    cache_values,
    q_weight,
    k_weight,
    v_weight,
    o_weight,
    gate_weight,
    up_weight,
    down_weight,
    attn_gain,
    post_attn_gain,
    ffn_gain,
    post_ffn_gain,
):
    blk, req = lax.axis_size("blk"), lax.axis_size("req")
    pairs = blk // 2
    b, r = lax.axis_index("blk"), lax.axis_index("req")
    x, core = b // 2, b % 2
    core_at = core[None].astype(jnp.int32)
    token_rows, features = hidden_states.shape
    req_count = context_lengths.shape[0]
    steps = token_rows // req_count
    _, slots, kv_count, size = cache_keys.shape
    part = token_rows // pairs

    def along_blk(value, to):
        return lax.ppermute(value, "blk", [(i, to(i)) for i in range(blk)])

    def to_core(value):
        return along_blk(value, lambda i: i ^ 1)

    def to_pair(value, hop):
        return along_blk(value, lambda i: (i // 2 + hop) % pairs * 2 + i % 2)

    def to_request(value, hop):
        return lax.ppermute(value, "req", [(i, (i + hop) % req) for i in range(req)])

    def own_rows(value, index):
        return lax.dynamic_slice_in_dim(value, index * part, part, 0)

    weights = fetch(q_weight, k_weight, v_weight)
    raised = (hidden_states.astype(jnp.float32) * attn_gain).astype(jnp.bfloat16)
    if blk == req and features == q_weight.shape[0]:
        turn = [(i * req + j, j * blk + i) for i in range(blk) for j in range(req)]
        moved = lax.ppermute(raised, ("blk", "req"), turn)
        gathered = lax.all_gather(moved, "blk", axis=0, tiled=True)
    else:
        rows = lax.all_gather(raised, "blk", axis=1, tiled=True)
        gathered = lax.all_to_all(rows, "req", split_axis=1, concat_axis=0, tiled=True)

    partial = project(r[None].astype(jnp.int32), gathered, *weights, req)
    hidden_states, post_attn_gain, partial = lax.optimization_barrier(
        (hidden_states, post_attn_gain, partial)
    )
    hops = sorted(range(1, req), key=lambda hop: -min(hop, req - hop))
    pieces = [partial[0]] + [to_request(partial[hop], hop) for hop in hops]

    states = hidden_states.astype(jnp.float32)
    local = jnp.sum(states * states, axis=1)
    if blk <= 4:
        total = local
        for hop in range(1, blk):
            total = total + along_blk(local, lambda i, hop=hop: (i + hop) % blk)
    else:
        total = lax.psum(local, "blk")
    total, cache_keys, cache_values, o_weight, gate_weight = lax.optimization_barrier(
        (total, cache_keys, cache_values, o_weight, gate_weight)
    )
    cache_keys, cache_values = fetch(
        cache_keys.reshape(req_count, slots * kv_count, size),
        cache_values.reshape(req_count, slots * kv_count, size),
    )
    (o_weight,) = fetch(o_weight)
    (gate_weight,) = fetch(gate_weight)
    gains = jnp.stack([post_attn_gain, ffn_gain, post_ffn_gain])
    held, held_gains = [], []
    for hop in range(pairs):
        to = lambda i, hop=hop: (i % pairs + hop) % pairs * 2 + i // pairs
        held.append(along_blk(own_rows(hidden_states, (b % pairs + hop) % pairs), to))
        held_gains.append(along_blk(gains, to))

    def in_order(list_of, axis):
        stacked = jnp.stack(list_of)
        return jnp.concatenate(
            [
                lax.dynamic_index_in_dim(stacked, (x + pairs - m) % pairs, 0, keepdims=False)
                for m in range(pairs)
            ],
            axis=axis,
        )

    residual = in_order(held, 1).astype(jnp.float32)
    post_attn_half, ffn_half, post_ffn_half = in_order(held_gains, 1)

    positions = (context_lengths[:, None] + jnp.arange(steps, dtype=jnp.int32)[None, :]).reshape(
        token_rows
    )
    cosine, sine = angles(positions, size)
    attended, new_keys, new_values = attend(
        context_lengths,
        pieces,
        scaling(total),
        cosine,
        sine,
        cache_keys,
        cache_values,
        kv_count,
    )
    draft_keys = new_keys.reshape(req_count, steps, kv_count, size)
    draft_values = new_values.reshape(req_count, steps, kv_count, size)

    passed = half_product(1 - core_at, attended, o_weight, jnp.bfloat16)
    passed = to_core(passed)
    kept = half_product(core_at, attended, o_weight, jnp.float32)
    both = kept + passed.astype(jnp.float32)
    mixed = own_rows(both, x)
    for hop in range(1, pairs):
        mixed = mixed + to_pair(
            own_rows(both, (x + hop) % pairs).astype(jnp.bfloat16), hop
        ).astype(jnp.float32)

    def row_total(value):
        own = jnp.sum(value * value, axis=1)
        return own + to_core(own)

    middle = (residual + mixed * scaling(row_total(mixed)) * post_attn_half).astype(jnp.bfloat16)
    middle_wide = middle.astype(jnp.float32)
    normed = (middle_wide * scaling(row_total(middle_wide)) * ffn_half).astype(jnp.bfloat16)

    normed, up_weight, down_weight = lax.optimization_barrier((normed, up_weight, down_weight))
    (up_weight,) = fetch(up_weight)
    (down_weight,) = fetch(down_weight)
    order = [0] + hops
    column = [normed] + [to_request(normed, hop) for hop in hops]
    columns = [column] + [
        [to_pair(block, hop) for block in column] for hop in range(1, pairs)
    ]
    hidden = []
    for blocks in columns:
        own = jnp.concatenate(blocks, axis=0)
        hidden.append(hidden_units(core_at, own, to_core(own), gate_weight, up_weight))

    back = []
    for hop in list(range(1, pairs)) + [0]:
        passed = to_core(half_product(1 - core_at, hidden[hop], down_weight, jnp.bfloat16))
        kept = half_product(core_at, hidden[hop], down_weight, jnp.float32)
        if hop:
            back.append(
                {
                    k: to_pair(
                        add_part([kept, passed], order.index(k), [], part, jnp.bfloat16),
                        pairs - hop,
                    )
                    for k in hops + [0]
                }
            )
    returned = [
        to_request(
            add_part([kept, passed], order.index(k), [b[k] for b in back], part, jnp.bfloat16),
            req - k,
        )
        for k in hops
    ]
    ffn_out = add_part([kept, passed], 0, [b[0] for b in back] + returned, part, jnp.float32)
    result = (middle_wide + ffn_out * scaling(row_total(ffn_out)) * post_ffn_half).astype(
        jnp.bfloat16
    )

    received = []
    for hop in range(pairs):
        to = lambda i, hop=hop: i % 2 * pairs + (i // 2 + hop) % pairs
        columns = lax.dynamic_slice_in_dim(result, (x + hop) % pairs * features, features, 1)
        received.append(along_blk(columns, to))
    stacked = jnp.stack(received)
    m = b % pairs
    layer_output = jnp.concatenate(
        [
            lax.dynamic_index_in_dim(stacked, (m + pairs - at) % pairs, 0, keepdims=False)
            for at in range(pairs)
        ],
        axis=0,
    )
    return (layer_output, draft_keys, draft_values)


def solution(mesh):
    placed = (
        P(("groups", "req"), "blk"),
        P(("groups", "req")),
        P(("groups", "req"), None, "blk", None),
        P(("groups", "req"), None, "blk", None),
        P("req", "blk"),
        P("req", "blk"),
        P("req", "blk"),
        P("blk", None),
        P(("blk", "req"), None),
        P(("blk", "req"), None),
        P(("blk", "req"), None),
        P("blk"),
        P("blk"),
        P("blk"),
        P("blk"),
    )
    return jax.shard_map(
        body,
        mesh=mesh,
        in_specs=placed,
        out_specs=(
            P(("groups", "req"), "blk"),
            P(("groups", "req"), None, "blk", None),
            P(("groups", "req"), None, "blk", None),
        ),
        check_vma=False,
    )
```

time: 344 us -> 180 us (0.52)
  waiting for transfers between devices: 198 us -> 50.5 us
  blocking collectives: 66 us -> 15.8 us
  Pallas kernels: 0 us -> 42.2 us
  matrix products: 39.9 us -> 0 us
  starting transfers between devices: 0.21 us -> 37.9 us
  between operations: 14.2 us -> 1.33 us
  local copies, waits for them, and re-layouts: 15.1 us -> 26.8 us
  other arithmetic: 9.58 us -> 5.02 us
    reduce_scatter x2 -> x0, waiting for transfers between devices: 73 us -> none  [the longest x1 50.5 us: body(): lax.psum_scatter(jnp.concatenate([jnp.dot(slices, q_weight, preferred_ele...]
    unnamed x7 -> x0, waiting for transfers between devices: 64.5 us -> none
    all_gather x1 -> x0, waiting for transfers between devices: 60.7 us -> none  [body(): piece = lax.all_gather(features, 'req', axis=0, tiled=True)]
    ppermute x0 -> x36, waiting for transfers between devices: none -> 50.5 us  [the longest x26 30.3 us: along_blk(): return lax.ppermute(value, 'blk', [(i, to(i)) for i in range(blk)])]
    pallas_call x0 -> x24, Pallas kernels: none -> 42.2 us  [the longest x2 16.7 us: hidden_units(): pl.pallas_call(functools.partial(hidden_kernel, block), in_specs=[pl.Bloc...]
    dot_general x11 -> x0, matrix products: 39.9 us -> none  [the longest x1 9.03 us: body(): lax.dot_general(piece, gate_weight, (((1,), (1,)), ((), ())), preferred_e...]
    ppermute x0 -> x36, starting transfers between devices: none -> 37.9 us  [the longest x26 22.2 us: along_blk(): return lax.ppermute(value, 'blk', [(i, to(i)) for i in range(blk)])]
    psum x4 -> x0, blocking collectives: 25.5 us -> none  [the longest x1 8.37 us: body(): total = lax.psum(jnp.sum(states * states, axis=1), 'blk')]
  transfers between devices with their start and end apart: 5 -> 36, of which waited for: 5 -> 16; matrix products, arithmetic and copies ran while one was open for 0% -> 4% of each run, Pallas kernels for 0% -> 16%
where the time goes in v1:
time: 180 us; the launch traced here: 179 us
  waiting for transfers between devices  50.5 us (28%)
  Pallas kernels  42.2 us (23%)
  starting transfers between devices  37.9 us (21%)
  local copies, waits for them, and re-layouts  26.8 us (15%)
  blocking collectives  15.8 us (9%)
  other arithmetic  5.02 us (3%)
    ppermute x26, waiting for transfers between devices, along_blk(): return lax.ppermute(value, 'blk', [(i, to(i)) for i in range(blk)])  30.3 us
    ppermute x26, starting transfers between devices, along_blk(): return lax.ppermute(value, 'blk', [(i, to(i)) for i in range(blk)])  22.2 us
    unnamed x52, local copies, waits for them, and re-layouts  22 us
    ppermute x9, waiting for transfers between devices, to_request(): lax.ppermute(value, 'req', [(i, (i + hop) % req) for i in range(req)])  20.2 us
    pallas_call x2, Pallas kernels, hidden_units(): pl.pallas_call(functools.partial(hidden_kernel, block), in_specs=[pl.Bloc...  16.7 us
    all_gather x1, blocking collectives, body(): gathered = lax.all_gather(moved, 'blk', axis=0, tiled=True)  15.8 us
    ppermute x9, starting transfers between devices, to_request(): lax.ppermute(value, 'req', [(i, (i + hop) % req) for i in range(req)])  15 us
    pallas_call x1, Pallas kernels, attend(): pl.pallas_call(functools.partial(attend_kernel, len(pieces), req_count, k...  10.3 us
  transfers between devices with their start and end apart: 36, of which 16 were waited for; matrix products, arithmetic and copies ran while one was open for 4% of the time, Pallas kernels for 16%

profile of v1, /device:TPU:0, one launch (start us, length us, event | category | flops | bytes accessed | tf_op | source)
XLA Modules:
  0.0 179.5 jit_solution(6274980232346233537)
XLA Ops:
  5.0 1.7 copy-done.11
  10.3 15.8 %all_gather.3.x_ref = bf16[320,1152]{1,0:T(8,128)(2,1)S(1)} all-gather(bf16[80,1152]{1,0:T(8,128)(2,1)S(1)} %collective-permute-done), channel_id=1, replica_groups=mesh['groups'=2,'blk'=4,'req'=4] {'blk'}, dimensions={0}, use_global_device_ids=true | all-gather | bytes 921600 | tf_op jit(solution)/shard_map/all_gather | solution.py:439
  26.2 1.9 %project.1 = (bf16[80,2048]{1,0:T(8,128)(2,1)S(1)}, bf16[80,2048]{1,0:T(8,128)(2,1)S(1)}, bf16[80,2048]{1,0:T(8,128)(2,1)S(1)}, bf16[80,2048]{1,0:T(8,128)(2,1)S(1)}) custom-call(s32[1]{0:T(128)} %bitcast.own_ref, bf16[320,1152]{1,0:T(8,128)(2,1)S(1)} %all_gather.3.x_ref, bf16[1152,1024]{1,0:T(8,128)(2,1)S(1)} %get-tuple-element.29.q_ref, ...), custom_call_target="tpu_custom_call" | custom-call | flops 1509949440 | bytes 4718592 | tf_op jit(solution)/shard_map/project/pallas_call | solution.py:120
  28.4 1.7 collective-permute-start.7
  31.4 2.8 %collective-permute-start.5 = (bf16[80,2048]{1,0:T(8,128)(2,1)S(1)}, bf16[80,2048]{1,0:T(8,128)(2,1)S(1)}, u32[]{:S(2)}, u32[]{:S(2)}) collective-permute-start(bf16[80,2048]{1,0:T(8,128)(2,1)S(1)} %get-tuple-element.40), channel_id=1, source_target_pairs={{0,3},{1,0},{2,1},{3,2},{4,7},{5,4},{6,5},{7,6},{8,11},{9,8},{10,9... | collective-permute-start | bytes 983048 | tf_op jit(solution)/shard_map/ppermute | solution.py:429
  34.3 3.4 %copy-done.10 = bf16[16,512,4,128]{3,2,1,0:T(4,128)(2,1)S(1)} copy-done((bf16[16,512,4,128]{3,2,1,0:T(4,128)(2,1)S(1)}, bf16[16,512,4,128]{3,2,1,0:T(4,128)(2,1)}, u32[]{:S(2)}) %copy-start.10) | copy-done | bytes 8388632
  38.9 3.3 %copy-done.2 = bf16[16,2048,128]{2,1,0:T(8,128)(2,1)} copy-done((bf16[16,2048,128]{2,1,0:T(8,128)(2,1)}, bf16[16,2048,128]{2,1,0:T(8,128)(2,1)S(1)}, u32[]{:S(2)}) %copy-start.2) | copy-done | bytes 8388632
  42.2 3.3 %copy-done.4 = bf16[16,2048,128]{2,1,0:T(8,128)(2,1)} copy-done((bf16[16,2048,128]{2,1,0:T(8,128)(2,1)}, bf16[16,2048,128]{2,1,0:T(8,128)(2,1)S(1)}, u32[]{:S(2)}) %copy-start.4) | copy-done | bytes 8388632
  45.6 3.7 %copy-done.1 = bf16[1024,4608]{1,0:T(8,128)(2,1)S(1)} copy-done((bf16[1024,4608]{1,0:T(8,128)(2,1)S(1)}, bf16[1024,4608]{1,0:T(8,128)(2,1)}, u32[]{:S(2)}) %copy-start.1) | copy-done | bytes 9437208
  49.9 4.9 %collective-permute-done.3.refs_2_ = bf16[80,2048]{1,0:T(8,128)(2,1)S(1)} collective-permute-done((bf16[80,2048]{1,0:T(8,128)(2,1)S(1)}, bf16[80,2048]{1,0:T(8,128)(2,1)S(1)}, u32[]{:S(2)}, u32[]{:S(2)}) %collective-permute-start.3) | collective-permute-done | bytes 327712 | tf_op jit(solution)/shard_map/ppermute | solution.py:429
  56.3 10.3 %attend.1 = (bf16[80,1024]{1,0:T(8,128)(2,1)S(1)}, bf16[80,512]{1,0:T(8,128)(2,1)S(1)}, bf16[80,512]{1,0:T(8,128)(2,1)S(1)}) custom-call(s32[16]{0:T(128)S(1)} %copy-done.8, bf16[80,2048]{1,0:T(8,128)(2,1)S(1)} %get-tuple-element.37.refs_1_, bf16[80,2048]{1,0:T(8,128)(2,1)S(1)} %collective-permute-done.3.refs_2_, ...), custom_call_target="tpu_custom_call" | custom-call | flops 1073741824 | bytes 16777216 | tf_op jit(solution)/shard_map/attend/pallas_call | solution.py:267
  68.5 3.4 %collective-permute-start.13 = (f32[3,1152]{1,0:T(4,128)S(1)}, f32[3,1152]{1,0:T(4,128)S(1)}, u32[]{:S(2)}, u32[]{:S(2)}) collective-permute-start(f32[3,1152]{1,0:T(4,128)S(1)} %pad_maximum_fusion.3), channel_id=1, source_target_pairs={{0,8},{4,0},{8,12},{12,4},{1,9},{5,1},{9,13},{13,5},{2,10},{6,2},{... | collective-permute-start | bytes 41480 | tf_op jit(solution)/shard_map/ppermute | solution.py:420
  72.7 1.7 collective-permute-start.2
  75.7 6.1 %collective-permute-done.10 = bf16[40,2304]{1,0:T(8,128)(2,1)S(1)} collective-permute-done((bf16[40,2304]{1,0:T(8,128)(2,1)S(1)}, bf16[40,2304]{1,0:T(8,128)(2,1)S(1)}, u32[]{:S(2)}, u32[]{:S(2)}) %collective-permute-start.10) | collective-permute-done | bytes 184352 | tf_op jit(solution)/shard_map/ppermute | solution.py:420
  84.9 5.6 %collective-permute-start.15 = (bf16[40,2304]{1,0:T(8,128)(2,1)S(1)}, bf16[40,2304]{1,0:T(8,128)(2,1)S(1)}, u32[]{:S(2)}, u32[]{:S(2)}) collective-permute-start(bf16[40,2304]{1,0:T(8,128)(2,1)S(1)} %fusion.2), channel_id=1, source_target_pairs={{0,2},{1,3},{2,0},{3,1},{4,6},{5,7},{6,4},{7,5},{8,10},{9,11},{10,... | collective-permute-start | bytes 552968 | tf_op jit(solution)/shard_map/ppermute | solution.py:429
  90.4 3.8 %collective-permute-start.17 = (bf16[40,2304]{1,0:T(8,128)(2,1)S(1)}, bf16[40,2304]{1,0:T(8,128)(2,1)S(1)}, u32[]{:S(2)}, u32[]{:S(2)}) collective-permute-start(bf16[40,2304]{1,0:T(8,128)(2,1)S(1)} %fusion.2), channel_id=1, source_target_pairs={{0,3},{1,0},{2,1},{3,2},{4,7},{5,4},{6,5},{7,6},{8,11},{9,8},{10,9... | collective-permute-start | bytes 552968 | tf_op jit(solution)/shard_map/ppermute | solution.py:429
  95.4 8.5 %collective-permute-done.15 = bf16[40,2304]{1,0:T(8,128)(2,1)S(1)} collective-permute-done((bf16[40,2304]{1,0:T(8,128)(2,1)S(1)}, bf16[40,2304]{1,0:T(8,128)(2,1)S(1)}, u32[]{:S(2)}, u32[]{:S(2)}) %collective-permute-start.15) | collective-permute-done | bytes 184352 | tf_op jit(solution)/shard_map/ppermute | solution.py:429
  107.1 4.2 %collective-permute-done.21 = bf16[40,2304]{1,0:T(8,128)(2,1)S(1)} collective-permute-done((bf16[40,2304]{1,0:T(8,128)(2,1)S(1)}, bf16[40,2304]{1,0:T(8,128)(2,1)S(1)}, u32[]{:S(2)}, u32[]{:S(2)}) %collective-permute-start.21) | collective-permute-done | bytes 184352 | tf_op jit(solution)/shard_map/ppermute | solution.py:420
  111.3 3.9 %collective-permute-done.22 = bf16[40,2304]{1,0:T(8,128)(2,1)S(1)} collective-permute-done((bf16[40,2304]{1,0:T(8,128)(2,1)S(1)}, bf16[40,2304]{1,0:T(8,128)(2,1)S(1)}, u32[]{:S(2)}, u32[]{:S(2)}) %collective-permute-start.22) | collective-permute-done | bytes 184352 | tf_op jit(solution)/shard_map/ppermute | solution.py:420
  115.3 2.3 %collective-permute-done.23 = bf16[40,2304]{1,0:T(8,128)(2,1)S(1)} collective-permute-done((bf16[40,2304]{1,0:T(8,128)(2,1)S(1)}, bf16[40,2304]{1,0:T(8,128)(2,1)S(1)}, u32[]{:S(2)}, u32[]{:S(2)}) %collective-permute-start.23) | collective-permute-done | bytes 184352 | tf_op jit(solution)/shard_map/ppermute | solution.py:420
  119.3 4.0 %copy-done = bf16[1152,4608]{1,0:T(8,128)(2,1)S(1)} copy-done((bf16[1152,4608]{1,0:T(8,128)(2,1)S(1)}, bf16[1152,4608]{1,0:T(8,128)(2,1)}, u32[]{:S(2)}) %copy-start) | copy-done | bytes 10616856
  124.2 8.3 %hidden_units.3.a_ref = bf16[9,160,128]{2,1,0:T(8,128)(2,1)S(1)} custom-call(s32[1]{0:T(128)} %bitcast.5.half_ref.core_ref, bf16[160,2304]{1,0:T(8,128)(2,1)S(1)} %constant_dynamic-update-slice_fusion.4.own_ref, bf16[160,2304]{1,0:T(8,128)(2,1)S(1)} %collective-permute-done.24.other_ref, bf16[1152,4608]{1,0:T(8,128)(2,1)S(1)} %fetch.9.gate_ref, ...), custom_call_target="tpu_custom_call" | custom-call | flops 3397386240 | bytes 21233664 | tf_op jit(solution)/shard_map/hidden_units/pallas_call | solution.py:376
  133.8 8.3 %hidden_units.2.a_ref = bf16[9,160,128]{2,1,0:T(8,128)(2,1)S(1)} custom-call(s32[1]{0:T(128)} %bitcast.5.half_ref.core_ref, bf16[160,2304]{1,0:T(8,128)(2,1)S(1)} %constant_dynamic-update-slice_fusion.own_ref, bf16[160,2304]{1,0:T(8,128)(2,1)S(1)} %collective-permute-done.18.other_ref, bf16[1152,4608]{1,0:T(8,128)(2,1)S(1)} %fetch.9.gate_ref, ...), custom_call_target="tpu_custom_call" | custom-call | flops 3397386240 | bytes 21233664 | tf_op jit(solution)/shard_map/hidden_units/pallas_call | solution.py:376
  150.7 2.0 %collective-permute-done.27.refs_2_ = bf16[40,2304]{1,0:T(8,128)(2,1)S(1)} collective-permute-done((bf16[40,2304]{1,0:T(8,128)(2,1)S(1)}, bf16[40,2304]{1,0:T(8,128)(2,1)S(1)}, u32[]{:S(2)}, u32[]{:S(2)}) %collective-permute-start.27) | collective-permute-done | bytes 184352 | tf_op jit(solution)/shard_map/ppermute | solution.py:420
  154.2 2.4 %collective-permute-done.29.refs_2_ = bf16[40,2304]{1,0:T(8,128)(2,1)S(1)} collective-permute-done((bf16[40,2304]{1,0:T(8,128)(2,1)S(1)}, bf16[40,2304]{1,0:T(8,128)(2,1)S(1)}, u32[]{:S(2)}, u32[]{:S(2)}) %collective-permute-start.29) | collective-permute-done | bytes 184352 | tf_op jit(solution)/shard_map/ppermute | solution.py:420
  156.7 3.8 %collective-permute-done.31.refs_2_ = bf16[40,2304]{1,0:T(8,128)(2,1)S(1)} collective-permute-done((bf16[40,2304]{1,0:T(8,128)(2,1)S(1)}, bf16[40,2304]{1,0:T(8,128)(2,1)S(1)}, u32[]{:S(2)}, u32[]{:S(2)}) %collective-permute-start.31) | collective-permute-done | bytes 184352 | tf_op jit(solution)/shard_map/ppermute | solution.py:420
  161.3 2.3 %collective-permute-done.26.refs_2_ = bf16[40,2304]{1,0:T(8,128)(2,1)S(1)} collective-permute-done((bf16[40,2304]{1,0:T(8,128)(2,1)S(1)}, bf16[40,2304]{1,0:T(8,128)(2,1)S(1)}, u32[]{:S(2)}, u32[]{:S(2)}) %collective-permute-start.26) | collective-permute-done | bytes 184352 | tf_op jit(solution)/shard_map/ppermute | solution.py:420
  163.6 3.0 %collective-permute-done.30.refs_4_ = bf16[40,2304]{1,0:T(8,128)(2,1)S(1)} collective-permute-done((bf16[40,2304]{1,0:T(8,128)(2,1)S(1)}, bf16[40,2304]{1,0:T(8,128)(2,1)S(1)}, u32[]{:S(2)}, u32[]{:S(2)}) %collective-permute-start.30) | collective-permute-done | bytes 184352 | tf_op jit(solution)/shard_map/ppermute | solution.py:429
  166.6 2.3 %collective-permute-done.32.refs_5_ = bf16[40,2304]{1,0:T(8,128)(2,1)S(1)} collective-permute-done((bf16[40,2304]{1,0:T(8,128)(2,1)}, bf16[40,2304]{1,0:T(8,128)(2,1)S(1)}, u32[]{:S(2)}, u32[]{:S(2)}) %collective-permute-start.32) | collective-permute-done | bytes 184352 | tf_op jit(solution)/shard_map/ppermute | solution.py:429
  172.2 2.5 %collective-permute-start.35 = (bf16[40,1152]{1,0:T(8,128)(2,1)S(1)}, bf16[40,1152]{1,0:T(8,128)(2,1)S(1)}, u32[]{:S(2)}, u32[]{:S(2)}) collective-permute-start(bf16[40,1152]{1,0:T(8,128)(2,1)S(1)} %get-tuple-element.62), channel_id=1, source_target_pairs={{0,4},{4,12},{8,0},{12,8},{1,5},{5,13},{9,1},{13,9},{2,6},{6,14},{... | collective-permute-start | bytes 276488 | tf_op jit(solution)/shard_map/ppermute | solution.py:420
  174.6 1.5 reshape.47
  176.2 1.5 reshape.48
  (154 shorter events, 43.8 us)
Async XLA Ops:
  1.7 8.7 %collective-permute-start = (bf16[80,1152]{1,0:T(8,128)(2,1)S(1)}, bf16[80,1152]{1,0:T(8,128)(2,1)S(1)}, u32[]{:S(2)}, u32[]{:S(2)}) collective-permute-start(bf16[80,1152]{1,0:T(8,128)(2,1)S(1)} %multiply_convert_fusion), channel_id=1, source_target_pairs={{0,0},{1,4},{2,8},{3,12},{4,1},{5,5},{6,9},{7,13},{8,2},{9,6},{10,... | collective-permute-start | bytes 552968 | tf_op jit(solution)/shard_map/ppermute | solution.py:438
  28.4 5.8 %collective-permute-start.7 = (f32[80]{0:T(128)S(1)}, f32[80]{0:T(128)S(1)}, u32[]{:S(2)}, u32[]{:S(2)}) collective-permute-start(f32[80]{0:T(128)S(1)} %multiply_reduce_fusion.2), channel_id=1, source_target_pairs={{0,8},{4,12},{8,0},{12,4},{1,9},{5,13},{9,1},{13,5},{2,10},{6,14},... | collective-permute-start | bytes 968 | tf_op jit(solution)/shard_map/ppermute | solution.py:420
  30.2 4.1 %collective-permute-start.6 = (f32[80]{0:T(128)S(1)}, f32[80]{0:T(128)S(1)}, u32[]{:S(2)}, u32[]{:S(2)}) collective-permute-start(f32[80]{0:T(128)S(1)} %multiply_reduce_fusion.2), channel_id=1, source_target_pairs={{0,4},{4,8},{8,12},{12,0},{1,5},{5,9},{9,13},{13,1},{2,6},{6,10},{... | collective-permute-start | bytes 968 | tf_op jit(solution)/shard_map/ppermute | solution.py:420
  30.2 24.6 %collective-permute-start.3 = (bf16[80,2048]{1,0:T(8,128)(2,1)S(1)}, bf16[80,2048]{1,0:T(8,128)(2,1)S(1)}, u32[]{:S(2)}, u32[]{:S(2)}) collective-permute-start(bf16[80,2048]{1,0:T(8,128)(2,1)S(1)} %get-tuple-element.38), channel_id=1, source_target_pairs={{0,2},{1,3},{2,0},{3,1},{4,6},{5,7},{6,4},{7,5},{8,10},{9,11},{10,... | collective-permute-start | bytes 983048 | tf_op jit(solution)/shard_map/ppermute | solution.py:429
  30.4 24.4 %collective-permute-start.4 = (bf16[80,2048]{1,0:T(8,128)(2,1)S(1)}, bf16[80,2048]{1,0:T(8,128)(2,1)S(1)}, u32[]{:S(2)}, u32[]{:S(2)}) collective-permute-start(bf16[80,2048]{1,0:T(8,128)(2,1)S(1)} %get-tuple-element.39), channel_id=1, source_target_pairs={{0,1},{1,2},{2,3},{3,0},{4,5},{5,6},{6,7},{7,4},{8,9},{9,10},{10,1... | collective-permute-start | bytes 983048 | tf_op jit(solution)/shard_map/ppermute | solution.py:429
  31.4 24.8 %collective-permute-start.5 = (bf16[80,2048]{1,0:T(8,128)(2,1)S(1)}, bf16[80,2048]{1,0:T(8,128)(2,1)S(1)}, u32[]{:S(2)}, u32[]{:S(2)}) collective-permute-start(bf16[80,2048]{1,0:T(8,128)(2,1)S(1)} %get-tuple-element.40), channel_id=1, source_target_pairs={{0,3},{1,0},{2,1},{3,2},{4,7},{5,4},{6,5},{7,6},{8,11},{9,8},{10,9... | collective-permute-start | bytes 983048 | tf_op jit(solution)/shard_map/ppermute | solution.py:429
  67.5 7.8 %collective-permute-start.9 = (bf16[80,2304]{1,0:T(8,128)(2,1)S(1)}, bf16[80,2304]{1,0:T(8,128)(2,1)S(1)}, u32[]{:S(2)}, u32[]{:S(2)}) collective-permute-start(bf16[80,2304]{1,0:T(8,128)(2,1)S(1)} %half_product.7), channel_id=1, source_target_pairs={{0,4},{4,0},{8,12},{12,8},{1,5},{5,1},{9,13},{13,9},{2,6},{6,2},{1... | collective-permute-start | bytes 1105928 | tf_op jit(solution)/shard_map/ppermute | solution.py:420
  67.7 7.8 %collective-permute-start.12 = (f32[3,1152]{1,0:T(4,128)S(1)}, f32[3,1152]{1,0:T(4,128)S(1)}, u32[]{:S(2)}, u32[]{:S(2)}) collective-permute-start(f32[3,1152]{1,0:T(4,128)S(1)} %pad_maximum_fusion.3), channel_id=1, source_target_pairs={{0,0},{4,8},{8,4},{12,12},{1,1},{5,9},{9,5},{13,13},{2,2},{6,10},{... | collective-permute-start | bytes 41480 | tf_op jit(solution)/shard_map/ppermute | solution.py:420
  68.5 7.0 %collective-permute-start.13 = (f32[3,1152]{1,0:T(4,128)S(1)}, f32[3,1152]{1,0:T(4,128)S(1)}, u32[]{:S(2)}, u32[]{:S(2)}) collective-permute-start(f32[3,1152]{1,0:T(4,128)S(1)} %pad_maximum_fusion.3), channel_id=1, source_target_pairs={{0,8},{4,0},{8,12},{12,4},{1,9},{5,1},{9,13},{13,5},{2,10},{6,2},{... | collective-permute-start | bytes 41480 | tf_op jit(solution)/shard_map/ppermute | solution.py:420
  72.0 10.1 %collective-permute-start.1 = (bf16[40,1152]{1,0:T(8,128)(2,1)S(1)}, bf16[40,1152]{1,0:T(8,128)(2,1)S(1)}, u32[]{:S(2)}, u32[]{:S(2)}) collective-permute-start(bf16[40,1152]{1,0:T(8,128)(2,1)S(1)} %get-tuple-element.67), channel_id=1, source_target_pairs={{0,0},{4,8},{8,4},{12,12},{1,1},{5,9},{9,5},{13,13},{2,2},{6,10},{... | collective-permute-start | bytes 276488 | tf_op jit(solution)/shard_map/ppermute | solution.py:420
  72.7 9.4 %collective-permute-start.2 = (bf16[40,1152]{1,0:T(8,128)(2,1)S(1)}, bf16[40,1152]{1,0:T(8,128)(2,1)S(1)}, u32[]{:S(2)}, u32[]{:S(2)}) collective-permute-start(bf16[40,1152]{1,0:T(8,128)(2,1)S(1)} %get-tuple-element.66), channel_id=1, source_target_pairs={{0,8},{4,0},{8,12},{12,4},{1,9},{5,1},{9,13},{13,5},{2,10},{6,2},{... | collective-permute-start | bytes 276488 | tf_op jit(solution)/shard_map/ppermute | solution.py:420
  75.5 6.3 %collective-permute-start.10 = (bf16[40,2304]{1,0:T(8,128)(2,1)S(1)}, bf16[40,2304]{1,0:T(8,128)(2,1)S(1)}, u32[]{:S(2)}, u32[]{:S(2)}) collective-permute-start(bf16[40,2304]{1,0:T(8,128)(2,1)S(1)} %dynamic-slice_convert_fusion), channel_id=1, source_target_pairs={{0,8},{4,12},{8,0},{12,4},{1,9},{5,13},{9,1},{13,5},{2,10},{6,14},... | collective-permute-start | bytes 552968 | tf_op jit(solution)/shard_map/ppermute | solution.py:420
  84.9 18.9 %collective-permute-start.15 = (bf16[40,2304]{1,0:T(8,128)(2,1)S(1)}, bf16[40,2304]{1,0:T(8,128)(2,1)S(1)}, u32[]{:S(2)}, u32[]{:S(2)}) collective-permute-start(bf16[40,2304]{1,0:T(8,128)(2,1)S(1)} %fusion.2), channel_id=1, source_target_pairs={{0,2},{1,3},{2,0},{3,1},{4,6},{5,7},{6,4},{7,5},{8,10},{9,11},{10,... | collective-permute-start | bytes 552968 | tf_op jit(solution)/shard_map/ppermute | solution.py:429
  90.4 14.5 %collective-permute-start.16 = (bf16[40,2304]{1,0:T(8,128)(2,1)S(1)}, bf16[40,2304]{1,0:T(8,128)(2,1)S(1)}, u32[]{:S(2)}, u32[]{:S(2)}) collective-permute-start(bf16[40,2304]{1,0:T(8,128)(2,1)S(1)} %fusion.2), channel_id=1, source_target_pairs={{0,1},{1,2},{2,3},{3,0},{4,5},{5,6},{6,7},{7,4},{8,9},{9,10},{10,1... | collective-permute-start | bytes 552968 | tf_op jit(solution)/shard_map/ppermute | solution.py:429
  90.4 15.4 %collective-permute-start.17 = (bf16[40,2304]{1,0:T(8,128)(2,1)S(1)}, bf16[40,2304]{1,0:T(8,128)(2,1)S(1)}, u32[]{:S(2)}, u32[]{:S(2)}) collective-permute-start(bf16[40,2304]{1,0:T(8,128)(2,1)S(1)} %fusion.2), channel_id=1, source_target_pairs={{0,3},{1,0},{2,1},{3,2},{4,7},{5,4},{6,5},{7,6},{8,11},{9,8},{10,9... | collective-permute-start | bytes 552968 | tf_op jit(solution)/shard_map/ppermute | solution.py:429
  94.2 12.8 %collective-permute-start.20 = (bf16[40,2304]{1,0:T(8,128)(2,1)S(1)}, bf16[40,2304]{1,0:T(8,128)(2,1)S(1)}, u32[]{:S(2)}, u32[]{:S(2)}) collective-permute-start(bf16[40,2304]{1,0:T(8,128)(2,1)S(1)} %fusion.2), channel_id=1, source_target_pairs={{0,8},{4,12},{8,0},{12,4},{1,9},{5,13},{9,1},{13,5},{2,10},{6,14},... | collective-permute-start | bytes 552968 | tf_op jit(solution)/shard_map/ppermute | solution.py:420
  103.8 7.5 %collective-permute-start.21 = (bf16[40,2304]{1,0:T(8,128)(2,1)S(1)}, bf16[40,2304]{1,0:T(8,128)(2,1)S(1)}, u32[]{:S(2)}, u32[]{:S(2)}) collective-permute-start(bf16[40,2304]{1,0:T(8,128)(2,1)S(1)} %collective-permute-done.15), channel_id=1, source_target_pairs={{0,8},{4,12},{8,0},{12,4},{1,9},{5,13},{9,1},{13,5},{2,10},{6,14},... | collective-permute-start | bytes 552968 | tf_op jit(solution)/shard_map/ppermute | solution.py:420
  104.9 10.4 %collective-permute-start.22 = (bf16[40,2304]{1,0:T(8,128)(2,1)S(1)}, bf16[40,2304]{1,0:T(8,128)(2,1)S(1)}, u32[]{:S(2)}, u32[]{:S(2)}) collective-permute-start(bf16[40,2304]{1,0:T(8,128)(2,1)S(1)} %collective-permute-done.16), channel_id=1, source_target_pairs={{0,8},{4,12},{8,0},{12,4},{1,9},{5,13},{9,1},{13,5},{2,10},{6,14},... | collective-permute-start | bytes 552968 | tf_op jit(solution)/shard_map/ppermute | solution.py:420
  105.9 11.7 %collective-permute-start.23 = (bf16[40,2304]{1,0:T(8,128)(2,1)S(1)}, bf16[40,2304]{1,0:T(8,128)(2,1)S(1)}, u32[]{:S(2)}, u32[]{:S(2)}) collective-permute-start(bf16[40,2304]{1,0:T(8,128)(2,1)S(1)} %collective-permute-done.17), channel_id=1, source_target_pairs={{0,8},{4,12},{8,0},{12,4},{1,9},{5,13},{9,1},{13,5},{2,10},{6,14},... | collective-permute-start | bytes 552968 | tf_op jit(solution)/shard_map/ppermute | solution.py:420
  117.6 6.6 %collective-permute-start.24 = (bf16[160,2304]{1,0:T(8,128)(2,1)S(1)}, bf16[160,2304]{1,0:T(8,128)(2,1)S(1)}, u32[]{:S(2)}, u32[]{:S(2)}) collective-permute-start(bf16[160,2304]{1,0:T(8,128)(2,1)S(1)} %constant_dynamic-update-slice_fusion.4.own_ref), channel_id=1, source_target_pairs={{0,4},{4,0},{8,12},{12,8},{1,5},{5,1},{9,13},{13,9},{2,6},{6,2},{1... | collective-permute-start | bytes 2211848 | tf_op jit(solution)/shard_map/ppermute | solution.py:420
  117.7 16.1 %collective-permute-start.18 = (bf16[160,2304]{1,0:T(8,128)(2,1)S(1)}, bf16[160,2304]{1,0:T(8,128)(2,1)S(1)}, u32[]{:S(2)}, u32[]{:S(2)}) collective-permute-start(bf16[160,2304]{1,0:T(8,128)(2,1)S(1)} %constant_dynamic-update-slice_fusion.own_ref), channel_id=1, source_target_pairs={{0,4},{4,0},{8,12},{12,8},{1,5},{5,1},{9,13},{13,9},{2,6},{6,2},{1... | collective-permute-start | bytes 2211848 | tf_op jit(solution)/shard_map/ppermute | solution.py:420
  133.7 11.3 %collective-permute-start.25 = (bf16[160,2304]{1,0:T(8,128)(2,1)S(1)}, bf16[160,2304]{1,0:T(8,128)(2,1)S(1)}, u32[]{:S(2)}, u32[]{:S(2)}) collective-permute-start(bf16[160,2304]{1,0:T(8,128)(2,1)S(1)} %half_product.11), channel_id=1, source_target_pairs={{0,4},{4,0},{8,12},{12,8},{1,5},{5,1},{9,13},{13,9},{2,6},{6,2},{1... | collective-permute-start | bytes 2211848 | tf_op jit(solution)/shard_map/ppermute | solution.py:420
  143.3 7.3 %collective-permute-start.19 = (bf16[160,2304]{1,0:T(8,128)(2,1)S(1)}, bf16[160,2304]{1,0:T(8,128)(2,1)S(1)}, u32[]{:S(2)}, u32[]{:S(2)}) collective-permute-start(bf16[160,2304]{1,0:T(8,128)(2,1)S(1)} %half_product.9), channel_id=1, source_target_pairs={{0,4},{4,0},{8,12},{12,8},{1,5},{5,1},{9,13},{13,9},{2,6},{6,2},{1... | collective-permute-start | bytes 2211848 | tf_op jit(solution)/shard_map/ppermute | solution.py:420
  145.0 7.6 %collective-permute-start.27 = (bf16[40,2304]{1,0:T(8,128)(2,1)S(1)}, bf16[40,2304]{1,0:T(8,128)(2,1)S(1)}, u32[]{:S(2)}, u32[]{:S(2)}) collective-permute-start(bf16[40,2304]{1,0:T(8,128)(2,1)S(1)} %add_part.9), channel_id=1, source_target_pairs={{0,8},{4,12},{8,0},{12,4},{1,9},{5,13},{9,1},{13,5},{2,10},{6,14},... | collective-permute-start | bytes 552968 | tf_op jit(solution)/shard_map/ppermute | solution.py:420
  146.2 10.3 %collective-permute-start.29 = (bf16[40,2304]{1,0:T(8,128)(2,1)S(1)}, bf16[40,2304]{1,0:T(8,128)(2,1)S(1)}, u32[]{:S(2)}, u32[]{:S(2)}) collective-permute-start(bf16[40,2304]{1,0:T(8,128)(2,1)S(1)} %add_part.11), channel_id=1, source_target_pairs={{0,8},{4,12},{8,0},{12,4},{1,9},{5,13},{9,1},{13,5},{2,10},{6,14},... | collective-permute-start | bytes 552968 | tf_op jit(solution)/shard_map/ppermute | solution.py:420
  147.3 13.2 %collective-permute-start.31 = (bf16[40,2304]{1,0:T(8,128)(2,1)S(1)}, bf16[40,2304]{1,0:T(8,128)(2,1)S(1)}, u32[]{:S(2)}, u32[]{:S(2)}) collective-permute-start(bf16[40,2304]{1,0:T(8,128)(2,1)S(1)} %add_part.13), channel_id=1, source_target_pairs={{0,8},{4,12},{8,0},{12,4},{1,9},{5,13},{9,1},{13,5},{2,10},{6,14},... | collective-permute-start | bytes 552968 | tf_op jit(solution)/shard_map/ppermute | solution.py:420
  149.6 13.9 %collective-permute-start.26 = (bf16[40,2304]{1,0:T(8,128)(2,1)S(1)}, bf16[40,2304]{1,0:T(8,128)(2,1)S(1)}, u32[]{:S(2)}, u32[]{:S(2)}) collective-permute-start(bf16[40,2304]{1,0:T(8,128)(2,1)S(1)} %add_part.8), channel_id=1, source_target_pairs={{0,8},{4,12},{8,0},{12,4},{1,9},{5,13},{9,1},{13,5},{2,10},{6,14},... | collective-permute-start | bytes 552968 | tf_op jit(solution)/shard_map/ppermute | solution.py:420
  152.7 10.9 %collective-permute-start.28 = (bf16[40,2304]{1,0:T(8,128)(2,1)S(1)}, bf16[40,2304]{1,0:T(8,128)(2,1)S(1)}, u32[]{:S(2)}, u32[]{:S(2)}) collective-permute-start(bf16[40,2304]{1,0:T(8,128)(2,1)S(1)} %add_part.10), channel_id=1, source_target_pairs={{0,2},{1,3},{2,0},{3,1},{4,6},{5,7},{6,4},{7,5},{8,10},{9,11},{10,... | collective-permute-start | bytes 552968 | tf_op jit(solution)/shard_map/ppermute | solution.py:429
  156.6 9.9 %collective-permute-start.30 = (bf16[40,2304]{1,0:T(8,128)(2,1)S(1)}, bf16[40,2304]{1,0:T(8,128)(2,1)S(1)}, u32[]{:S(2)}, u32[]{:S(2)}) collective-permute-start(bf16[40,2304]{1,0:T(8,128)(2,1)S(1)} %add_part.12), channel_id=1, source_target_pairs={{0,3},{1,0},{2,1},{3,2},{4,7},{5,4},{6,5},{7,6},{8,11},{9,8},{10,9... | collective-permute-start | bytes 552968 | tf_op jit(solution)/shard_map/ppermute | solution.py:429
  161.3 7.6 %collective-permute-start.32 = (bf16[40,2304]{1,0:T(8,128)(2,1)}, bf16[40,2304]{1,0:T(8,128)(2,1)S(1)}, u32[]{:S(2)}, u32[]{:S(2)}) collective-permute-start(bf16[40,2304]{1,0:T(8,128)(2,1)} %add_part.14), channel_id=1, source_target_pairs={{0,1},{1,2},{2,3},{3,0},{4,5},{5,6},{6,7},{7,4},{8,9},{9,10},{10,1... | collective-permute-start | bytes 552968 | tf_op jit(solution)/shard_map/ppermute | solution.py:429
  171.5 6.2 %collective-permute-start.34 = (bf16[40,1152]{1,0:T(8,128)(2,1)S(1)}, bf16[40,1152]{1,0:T(8,128)(2,1)S(1)}, u32[]{:S(2)}, u32[]{:S(2)}) collective-permute-start(bf16[40,1152]{1,0:T(8,128)(2,1)S(1)} %get-tuple-element.63), channel_id=1, source_target_pairs={{0,0},{4,8},{8,4},{12,12},{1,1},{5,9},{9,5},{13,13},{2,2},{6,10},{... | collective-permute-start | bytes 276488 | tf_op jit(solution)/shard_map/ppermute | solution.py:420
  172.2 6.5 %collective-permute-start.35 = (bf16[40,1152]{1,0:T(8,128)(2,1)S(1)}, bf16[40,1152]{1,0:T(8,128)(2,1)S(1)}, u32[]{:S(2)}, u32[]{:S(2)}) collective-permute-start(bf16[40,1152]{1,0:T(8,128)(2,1)S(1)} %get-tuple-element.62), channel_id=1, source_target_pairs={{0,4},{4,12},{8,0},{12,8},{1,5},{5,13},{9,1},{13,9},{2,6},{6,14},{... | collective-permute-start | bytes 276488 | tf_op jit(solution)/shard_map/ppermute | solution.py:420
  (27 other events, 396.2 us)
